TPU v7x, 32 devices: a whole 2x2x4 slice. The times are simulated.
32 devices in a mesh: gx: 8 (over z, core), gy: 4 (over y, x).
Axes of the slice: x: 2, y: 2, z: 4, core: 2. Of those that a mesh axis runs over, the one named last changes fastest.
Arguments:
- tokens: bfloat16 [512, 4096], P('gx', 'gy'), may hold values from -6 to 6
- gate_blocks: bfloat16 [4, 8, 84, 128, 128], P('gy', 'gx'), may hold values from -0.125 to 0.125
- up_blocks: bfloat16 [4, 8, 84, 128, 128], P('gy', 'gx'), may hold values from -0.125 to 0.125
- gate_coords: int32 [4, 8, 84, 2], P('gy', 'gx'), may hold values from 0 to 13, as said below
- gate_count: int32 [4, 8], P('gy', 'gx'), may hold values from 28 to 84, as said below
- down_blocks: bfloat16 [8, 4, 48, 128, 128], P('gx', 'gy'), may hold values from -0.09375 to 0.09375
- down_rows: int32 [8, 4, 8], P('gx'), may hold values from 0 to 13, as said below
- down_coords: int32 [8, 4, 48, 2], P('gx', 'gy'), may hold values from 0 to 7, as said below
- down_count: int32 [8, 4], P('gx', 'gy'), may hold values from 16 to 48, as said below
Outputs:
- mixed: bfloat16 [512, 4096], P('gx', 'gy')
Inputs may be any that keep to these rules, and one draw needn't show every extreme that they name: `gate_coords`: within each tile the 84 (model-width block, hidden block) pairs are distinct, the first below 8, the second below 14; only the first gate_count slots are live. `gate_count`: some tile has all 84 slots live. `down_rows`: within each down tile the 8 hidden blocks are distinct. `down_coords`: within each down tile the 48 (kept-row index below 8, model-width block below 8) pairs are distinct; only the first down_count slots are live. `down_count`: some tile has all 48 slots live.
All inputs are finite; a program needn't handle non-finite values.
Results may differ from a plain program's by a relative error of at most 0.025.
Values may be sent and summed in bfloat16 or wider, within the bound.
A program may use at most 64 MiB of HBM per device.

v0:
```python
import functools

import jax
import jax.numpy as jnp
from jax import lax
from jax.experimental import pallas as pl
from jax.experimental.pallas import tpu as pltpu
from jax.sharding import PartitionSpec as P

BLOCK = 128
FF = 14336
MESH = pl.DeviceIdType.MESH
F32, BF16 = jnp.float32, jnp.bfloat16


def factor(n):
    low = 1
    while low * low * 4 <= n and n % (low * 2) == 0:
        low *= 2
    return n // low, low


def kernel(cfg, tab, downs, kept, tok, gblk, ublk, dblk, out, gw, uw, dw, gat, pa, pb,
           r1a, r1b, s2a, s2b, r2a, r2b, acca, accb, hid, a2s, a2r, ps, fp, f2, fr, facc,
           lsem, gs, gr, s1as, s1ar, s1bs, s1br, s2as, s2ar, s2bs, s2br, xs, xr, fs, fq, fps, fpr):
    n_gx, n_gy, n_hi, n_lo, per, nc, rp, rows, n_model, fb, ca, cap, used, capd = cfg
    gx, gy = lax.axis_index("gx"), lax.axis_index("gy")
    zc, mc = gx // per, gx % per
    hi, lo = gy // n_lo, gy % n_lo
    loads = [
        pltpu.make_async_copy(gblk, gw.at[pl.ds(0, cap)], lsem.at[0]),
        pltpu.make_async_copy(ublk, uw.at[pl.ds(0, cap)], lsem.at[1]),
        pltpu.make_async_copy(dblk, dw.at[pl.ds(0, capd)], lsem.at[2]),
    ]
    for load in loads:
        load.start()
    barrier = pltpu.get_barrier_semaphore()
    for d in range(1, n_gy):
        pl.semaphore_signal(barrier, inc=1, device_id=(gx, (gy + d) % n_gy), device_id_type=MESH)
    for d in range(1, n_gx):
        pl.semaphore_signal(barrier, inc=1, device_id=((gx + d) % n_gx, gy), device_id_type=MESH)
    pl.semaphore_wait(barrier, n_gy + n_gx - 2)

    sends = []

    def send(src, dst, ssem, rsem, dev):
        copy = pltpu.make_async_remote_copy(
            src_ref=src, dst_ref=dst, send_sem=ssem, recv_sem=rsem,
            device_id=dev, device_id_type=MESH)
        copy.start()
        sends.append(copy)

    def arrived(ref, sem):
        pltpu.make_async_remote_copy(
            src_ref=ref, dst_ref=ref, send_sem=sem, recv_sem=sem,
            device_id=((gx + 1) % n_gx, gy), device_id_type=MESH).wait_recv()

    order = list(range(nc))
    for j in range(1, per):
        send(tok, gat.at[0, mc], gs.at[0, j], gr.at[0, mc], (zc * per + (mc + j) % per, gy))
    for o in order:
        if o:
            send(tok, gat.at[o, mc], gs.at[o, 0], gr.at[o, mc], ((zc ^ o) * per + mc, gy))
    gat[0, mc] = tok[...]

    def relay(o):
        if o:
            arrived(gat.at[o, mc], gr.at[o, mc])
            for j in range(1, per):
                send(gat.at[o, mc], gat.at[o, mc], gs.at[o, j], gr.at[o, mc],
                     (zc * per + (mc + j) % per, gy))

    gw[cap] = jnp.zeros((BLOCK, BLOCK), BF16)
    uw[cap] = jnp.zeros((BLOCK, BLOCK), BF16)
    dw[capd] = jnp.zeros((BLOCK, BLOCK), BF16)
    loads[0].wait()
    loads[1].wait()

    tall = per * rows

    def project(k):
        for j in range(1, per):
            c = (mc + j) % per
            arrived(gat.at[k, c], gr.at[k, c])
        for part, first, many in ((pa, 0, ca), (pb, ca, fb - ca)):
            def col(c, _, part=part, first=first):
                to = pl.multiple_of(c * 2 * BLOCK, 2 * BLOCK)
                slots = [tab[r * fb + c + first] for r in range(n_model)]
                weight = jnp.concatenate(
                    [jnp.concatenate([gw[i], uw[i]], axis=1) for i in slots], axis=0)
                y = jnp.dot(gat[k].reshape(tall, n_model * BLOCK), weight,
                            preferred_element_type=F32)
                part[k, :, :, :, pl.ds(to, 2 * BLOCK)] = y.astype(BF16).reshape(
                    n_hi, n_lo, rp, 2 * BLOCK)
                return 0

            lax.fori_loop(0, many, col, 0, unroll=True)
            if part is pa:
                for d in range(1, n_lo):
                    l2 = (lo + d) % n_lo
                    send(pa.at[k, :, l2], r1a.at[k, d - 1], s1as.at[k, d - 1],
                         s1ar.at[k, d - 1], (gx, hi * n_lo + l2))
            else:
                for d in range(1, n_hi):
                    h2 = (hi + d) % n_hi
                    send(pb.at[k, h2], r1b.at[k, d - 1], s1bs.at[k, d - 1],
                         s1br.at[k, d - 1], (gx, h2 * n_lo + lo))

    def reduce_first(k):
        for d in range(1, n_lo):
            arrived(r1a.at[k, d - 1], s1ar.at[k, d - 1])
        for e in list(range(1, n_hi)) + [0]:
            h2 = (hi + e) % n_hi
            s = pa[k, h2, lo].astype(F32)
            for d in range(1, n_lo):
                s = s + r1a[k, d - 1, h2].astype(F32)
            if e == 0:
                acca[k] = s
            else:
                s2a[k, e - 1] = s.astype(BF16)
                send(s2a.at[k, e - 1], r2a.at[k, e - 1], s2as.at[k, e - 1],
                     s2ar.at[k, e - 1], (gx, h2 * n_lo + lo))
        for d in range(1, n_hi):
            arrived(r1b.at[k, d - 1], s1br.at[k, d - 1])
        for e in list(range(1, n_lo)) + [0]:
            l2 = (lo + e) % n_lo
            s = pb[k, hi, l2].astype(F32)
            for d in range(1, n_hi):
                s = s + r1b[k, d - 1, l2].astype(F32)
            if e == 0:
                accb[k] = s
            else:
                s2b[k, e - 1] = s.astype(BF16)
                send(s2b.at[k, e - 1], r2b.at[k, e - 1], s2bs.at[k, e - 1],
                     s2br.at[k, e - 1], (gx, hi * n_lo + l2))

    def activate(k):
        for d in range(1, n_hi):
            arrived(r2a.at[k, d - 1], s2ar.at[k, d - 1])
        for d in range(1, n_lo):
            arrived(r2b.at[k, d - 1], s2br.at[k, d - 1])
        for c in range(fb):
            acc, got, peers, at = (
                (acca, r2a, n_hi, c) if c < ca else (accb, r2b, n_lo, c - ca))
            cols = pl.ds(at * 2 * BLOCK, 2 * BLOCK)
            s = acc[k, :, cols]
            for d in range(1, peers):
                s = s + got[k, d - 1, :, cols].astype(F32)
            gate, up = s[:, :BLOCK], s[:, BLOCK:]
            hid[c] = (gate / (1.0 + jnp.exp(-gate)) * up).astype(BF16)
        for d in list(range(1, n_gy)) + [0]:
            dest = (gy + d) % n_gy
            for q in range(used):
                row = kept[0, dest, q]
                cols = pl.ds(q * BLOCK, BLOCK)
                if d == 0:
                    a2r[k, 0, :, cols] = hid[row]
                else:
                    a2s[k, d - 1, :, cols] = hid[row]
            if d:
                send(a2s.at[k, d - 1], a2r.at[k, d], xs.at[k, d - 1],
                     xr.at[k, d - 1], (gx, dest))

    wide = 2 * BLOCK

    def mix(k):
        for d in range(1, n_gy):
            arrived(a2r.at[k, d], xr.at[k, d - 1])

        def col(c, _):
            at = pl.multiple_of(c * wide, wide)
            slots = [[downs[r * n_model + c * 2 + i] for i in range(2)]
                     for r in range(used)]
            weight = jnp.concatenate(
                [jnp.concatenate([dw[i] for i in pair], axis=1) for pair in slots], axis=0)
            y = jnp.dot(a2r[k].reshape(n_gy * rp, used * BLOCK), weight,
                        preferred_element_type=F32).astype(BF16)
            for d in range(n_gy):
                own = (gy + n_gy - d) % n_gy
                ps[k, pl.ds(pl.multiple_of(own * rp, rp), rp), pl.ds(at, wide)] = (
                    y[d * rp:(d + 1) * rp])
            return 0

        lax.fori_loop(0, n_model * BLOCK // wide, col, 0)
        for j in range(1, per):
            cj = (mc + j) % per
            send(ps.at[k, pl.ds(pl.multiple_of(cj * rows, rows), rows)], fp.at[k, j - 1],
                 fps.at[k, j - 1], fpr.at[k, j - 1], (zc * per + cj, gy))

    def finish(k):
        s = ps[k, pl.ds(pl.multiple_of(mc * rows, rows), rows)].astype(F32)
        for j in range(1, per):
            arrived(fp.at[k, j - 1], fpr.at[k, j - 1])
            s = s + fp[k, j - 1].astype(F32)
        if k:
            f2[k] = s.astype(BF16)
            send(f2.at[k], fr.at[k], fs.at[k], fq.at[k], ((zc ^ k) * per + mc, gy))
        else:
            facc[...] = s

    relay(order[0])
    for s in range(nc + 4):
        if s < nc:
            project(order[s])
        if s + 1 < nc:
            relay(order[s + 1])
        if s == 0:
            loads[2].wait()
        if 0 <= s - 1 < nc:
            reduce_first(order[s - 1])
        if 0 <= s - 4 < nc:
            finish(order[s - 4])
        if 0 <= s - 2 < nc:
            activate(order[s - 2])
        if 0 <= s - 3 < nc:
            mix(order[s - 3])

    for k in order:
        if k:
            arrived(fr.at[k], fq.at[k])
            facc[...] += fr[k].astype(F32)
    out[...] = facc[...].astype(BF16)
    for copy in sends:
        copy.wait_send()


def inverse(coords, count, row_count, col_count):
    slots = coords.shape[0]
    slot = jnp.arange(slots, dtype=jnp.int32)
    place = coords[:, 0] * col_count + coords[:, 1]
    spot = jnp.arange(row_count * col_count, dtype=jnp.int32)
    hit = (place[:, None] == spot[None, :]) & (slot < count)[:, None]
    return jnp.min(jnp.where(hit, slot[:, None], slots), axis=0)


def solution(mesh):
    n_gx, n_gy = mesh.shape["gx"], mesh.shape["gy"]
    n_hi, n_lo = factor(n_gy)
    per = 2 if n_gx % 2 == 0 else 1
    nc = n_gx // per

    def body(tokens, gate_blocks, up_blocks, gate_coords, gate_count,
             down_blocks, down_rows, down_coords, down_count):
        rows, width = tokens.shape
        n_model = width // BLOCK
        fb = FF // (BLOCK * n_gx)
        ca = (fb + 1) // 2
        cb = fb - ca
        cap, capd, used = gate_blocks.shape[2], down_blocks.shape[2], down_rows.shape[-1]
        rp = per * rows // n_gy
        tab = inverse(gate_coords[0, 0], gate_count[0, 0], n_model, fb)
        downs = inverse(down_coords[0, 0], down_count[0, 0], used, n_model)
        cfg = (n_gx, n_gy, n_hi, n_lo, per, nc, rp, rows, n_model, fb, ca, cap, used, capd)
        wa, wb = ca * 2 * BLOCK, cb * 2 * BLOCK
        kl, kh, kg = max(n_lo - 1, 1), max(n_hi - 1, 1), max(n_gy - 1, 1)
        vm, dma = pltpu.VMEM, pltpu.SemaphoreType.DMA
        hbm = pl.BlockSpec(memory_space=pltpu.HBM)
        return pl.pallas_call(
            functools.partial(kernel, cfg),
            out_shape=jax.ShapeDtypeStruct((rows, width), BF16),
            in_specs=[
                pl.BlockSpec(memory_space=pltpu.SMEM),
                pl.BlockSpec(memory_space=pltpu.SMEM),
                pl.BlockSpec(memory_space=pltpu.SMEM),
                pl.BlockSpec(memory_space=pltpu.VMEM),
                hbm, hbm, hbm,
            ],
            out_specs=pl.BlockSpec(memory_space=pltpu.VMEM),
            scratch_shapes=[
                vm((cap + 1, BLOCK, BLOCK), BF16),
                vm((cap + 1, BLOCK, BLOCK), BF16),
                vm((capd + 1, BLOCK, BLOCK), BF16),
                vm((nc, per, rows, width), BF16),
                vm((nc, n_hi, n_lo, rp, wa), BF16),
                vm((nc, n_hi, n_lo, rp, wb), BF16),
                vm((nc, kl, n_hi, rp, wa), BF16),
                vm((nc, kh, n_lo, rp, wb), BF16),
                vm((nc, kh, rp, wa), BF16),
                vm((nc, kl, rp, wb), BF16),
                vm((nc, kh, rp, wa), BF16),
                vm((nc, kl, rp, wb), BF16),
                vm((nc, rp, wa), F32),
                vm((nc, rp, wb), F32),
                vm((fb, rp, BLOCK), BF16),
                vm((nc, kg, rp, used * BLOCK), BF16),
                vm((nc, n_gy, rp, used * BLOCK), BF16),
                vm((nc, per * rows, width), BF16),
                vm((nc, max(per - 1, 1), rows, width), BF16),
                vm((nc, rows, width), BF16),
                vm((nc, rows, width), BF16),
                vm((rows, width), F32),
                dma((3,)),
                dma((nc, per)), dma((nc, per)),
                dma((nc, kl)), dma((nc, kl)),
                dma((nc, kh)), dma((nc, kh)),
                dma((nc, kh)), dma((nc, kh)),
                dma((nc, kl)), dma((nc, kl)),
                dma((nc, kg)), dma((nc, kg)),
                dma((nc,)), dma((nc,)),
                dma((nc, max(per - 1, 1))), dma((nc, max(per - 1, 1))),
            ],
            compiler_params=pltpu.CompilerParams(
                collective_id=0, has_side_effects=True, vmem_limit_bytes=60 * 1024 * 1024),
        )(tab, downs, down_rows, tokens, gate_blocks.reshape(cap, BLOCK, BLOCK),
          up_blocks.reshape(cap, BLOCK, BLOCK), down_blocks.reshape(capd, BLOCK, BLOCK))

    return jax.shard_map(
        body,
        mesh=mesh,
        in_specs=(
            P("gx", "gy"),
            P("gy", "gx", None, None, None),
            P("gy", "gx", None, None, None),
            P("gy", "gx", None, None),
            P("gy", "gx"),
            P("gx", "gy", None, None, None),
            P("gx", None, None),
            P("gx", "gy", None, None),
            P("gx", "gy"),
        ),
        out_specs=P("gx", "gy"),
        check_vma=False,
    )
```

profile of v0, /device:TPU:0, one launch (start us, length us, event | category | flops | bytes accessed | tf_op | source)
XLA Modules:
  0.0 68.7 jit_solution(7188546672986369437)
XLA Ops:
  1.3 0.8 %add_bitcast_fusion.1 = s32[84]{0:T(128)S(1)} fusion(s32[84,2]{0,1:T(2,128)} %bitcast.16), kind=kLoop, calls=%fused_computation.9 | loop fusion | flops 168 | bytes 1008 | tf_op jit(solution)/shard_map/eq | solution.py:232
  2.1 0.6 select_reduce_fusion.tab
  2.7 0.8 %add_bitcast_fusion = s32[48]{0:T(128)S(1)} fusion(s32[48,2]{0,1:T(2,128)} %bitcast.17), kind=kLoop, calls=%fused_computation.7 | loop fusion | flops 96 | bytes 576 | tf_op jit(solution)/shard_map/eq | solution.py:232
  3.5 0.6 select_reduce_fusion.1.downs
  4.1 63.1 %shard_map.91 = bf16[64,1024]{1,0:T(8,128)(2,1)} custom-call(s32[112]{0:T(128)} %select_reduce_fusion.tab, s32[64]{0:T(128)} %select_reduce_fusion.1.downs, s32[1,4,8]{2,1,0:T(4,128)} %kept.1, bf16[64,1024]{1,0:T(8,128)(2,1)} %tok.1, bf16[84,128,128]{2,1,0:T(8,128)(2,1)} %bitcast.13, bf16[84,128,128]{2,1,0:T(8,128)(2,1)} %bitcast.14, ...), custom_call_target="tpu_custom_call" | custom-call | tf_op jit(solution)/shard_map/pallas_call | solution.py:258
  67.2 1.6 %copy.13 = bf16[64,1024]{1,0:T(8,128)(2,1)} copy(bf16[64,1024]{1,0:T(8,128)(2,1)} %shard_map.91) | data formatting | bytes 262144
  (2 shorter events, 0.0 us)
where the time goes:
time: 69.8 us; the launch traced here: 68.7 us
  Pallas kernels  63.1 us (90%)
  other arithmetic  2.75 us (4%)
  local copies, waits for them, and re-layouts  1.57 us (2%)
  between operations  1.32 us (2%)
    pallas_call x1, Pallas kernels, body(): pl.pallas_call(functools.partial(kernel, cfg), out_shape=jax.ShapeDtypeSt...  63.1 us
    unnamed x1, local copies, waits for them, and re-layouts  1.57 us
    eq x2, other arithmetic, inverse(): hit = (place[:, None] == spot[None, :]) & (slot < count)[:, None]  1.52 us

commit v1 on v0

v1 whole, which is shorter than its diff:
```python
import functools

import jax
import jax.numpy as jnp
from jax import lax
from jax.experimental import pallas as pl
from jax.experimental.pallas import tpu as pltpu
from jax.sharding import PartitionSpec as P

BLOCK = 128
LANES = 128
FF = 14336
MESH = pl.DeviceIdType.MESH
F32, BF16, I32 = jnp.float32, jnp.bfloat16, jnp.int32


def factor(n):
    low = 1
    while low * low * 4 <= n and n % (low * 2) == 0:
        low *= 2
    return n // low, low


def kernel(cfg, gco_h, gct_h, dco_h, dct_h, kept_h, tok, gblk, ublk, dblk, out,
           gco, gct, dco, dct, kept, tabv, tabs,
           gw, uw, dw, gat, pa, pb,
           r1a, r1b, s2a, s2b, r2a, r2b, acca, accb, hid, a2s, a2r, ps, fp, f2, fr, facc,
           lsem, gs, gr, s1as, s1ar, s1bs, s1br, s2as, s2ar, s2bs, s2br, xs, xr, fs, fq, fps, fpr):
    (n_gx, n_gy, n_hi, n_lo, per, nc, halves, rp, hr, n_model, fb, ca,
     cap, used, capd) = cfg
    gx, gy = lax.axis_index("gx"), lax.axis_index("gy")
    zc, mc = gx // per, gx % per
    hi, lo = gy // n_lo, gy % n_lo
    tall = per * hr
    down_at = -(-n_model * fb // LANES)

    barrier = pltpu.get_barrier_semaphore()

    def greet(dev):
        pl.semaphore_signal(barrier, inc=1, device_id=dev, device_id_type=MESH)

    for d in range(1, n_lo):
        greet((gx, hi * n_lo + (lo + d) % n_lo))
    for d in range(1, n_hi):
        greet((gx, (hi + d) % n_hi * n_lo + lo))
    for d in range(1, per):
        greet((zc * per + (mc + d) % per, gy))

    @pl.when(zc > 0)
    def _():
        greet(((zc - 1) * per + mc, gy))

    @pl.when(zc < nc - 1)
    def _():
        greet(((zc + 1) * per + mc, gy))

    smalls = [
        pltpu.make_async_copy(gco_h, gco, lsem.at[0]),
        pltpu.make_async_copy(gct_h, gct, lsem.at[1]),
        pltpu.make_async_copy(dco_h, dco, lsem.at[2]),
        pltpu.make_async_copy(dct_h, dct, lsem.at[3]),
        pltpu.make_async_copy(kept_h, kept, lsem.at[4]),
    ]
    mine = [
        pltpu.make_async_copy(tok.at[pl.ds(h * hr, hr)], gat.at[zc, h, mc], lsem.at[8 + h])
        for h in range(halves)
    ]
    loads = [
        pltpu.make_async_copy(gblk, gw.at[pl.ds(0, cap)], lsem.at[5]),
        pltpu.make_async_copy(ublk, uw.at[pl.ds(0, cap)], lsem.at[6]),
        pltpu.make_async_copy(dblk, dw.at[pl.ds(0, capd)], lsem.at[7]),
    ]
    for load in smalls + mine + loads:
        load.start()

    def table(coords, count, slots, inner, spots, first):
        wide = -(-spots // LANES)
        lane = lax.broadcasted_iota(I32, (1, LANES), 1)
        row = [jnp.full((1, LANES), slots, I32) for _ in range(wide)]
        live = count[0, 0]
        for s in range(slots):
            place = coords[0, s] * inner + coords[1, s]
            place = jnp.where(s < live, place, -1)
            for w in range(wide):
                row[w] = jnp.where(lane + w * LANES == place, s, row[w])
        for w in range(wide):
            tabv[first + w] = row[w]

    with jax.named_scope("tables"):
        for load in smalls:
            load.wait()
        table(gco, gct, cap, fb, n_model * fb, 0)
        table(dco, dct, capd, n_model, used * n_model, down_at)
        gw[cap] = jnp.zeros((BLOCK, BLOCK), BF16)
        uw[cap] = jnp.zeros((BLOCK, BLOCK), BF16)
        dw[capd] = jnp.zeros((BLOCK, BLOCK), BF16)
        tables = pltpu.make_async_copy(tabv, tabs, lsem.at[0])
        tables.start()
        for load in mine:
            load.wait()

    with jax.named_scope("barrier"):
        pl.semaphore_wait(
            barrier,
            n_lo + n_hi + per - 3 + jnp.minimum(zc, 1) + jnp.minimum(nc - 1 - zc, 1))

    sends = []

    def send(src, dst, ssem, rsem, dev, when=None):
        copy = pltpu.make_async_remote_copy(
            src_ref=src, dst_ref=dst, send_sem=ssem, recv_sem=rsem,
            device_id=dev, device_id_type=MESH)
        if when is None:
            copy.start()
        else:
            pl.when(when)(copy.start)
        sends.append((copy, when))

    def arrived(ref, sem):
        with jax.named_scope("w"):
            pltpu.make_async_remote_copy(
                src_ref=ref, dst_ref=ref, send_sem=sem, recv_sem=sem,
                device_id=(gx, (gy + 1) % n_gy), device_id_type=MESH).wait_recv()

    def share(c, h, up, down, there=None):
        def both(a, b):
            return b if a is None else a & b
        ref = gat.at[c, h, mc]
        if up:
            send(ref, ref, gs.at[c, h, 0], gr.at[c, h, mc], ((zc + 1) * per + mc, gy),
                 both(there, zc < nc - 1))
        if down:
            send(ref, ref, gs.at[c, h, 1], gr.at[c, h, mc], ((zc - 1) * per + mc, gy),
                 both(there, zc > 0))
        for j in range(1, per):
            send(ref, ref, gs.at[c, h, 1 + j], gr.at[c, h, mc],
                 (zc * per + (mc + j) % per, gy), there)

    def relay(d, h):
        for c, there, up in ((zc - d, zc >= d, True), (zc + d, zc < nc - d, False)):
            @pl.when(there)
            def _(c=c):
                arrived(gat.at[c, h, mc], gr.at[c, h, mc])

            share(c, h, up, not up, there)

    jobs = [(k, h) for k in range(nc) for h in range(halves)]
    number = {job: i for i, job in enumerate(jobs)}

    def project(job):
        j, (k, h) = number[job], job
        chip = zc ^ k
        for d in range(1, per):
            c = (mc + d) % per
            arrived(gat.at[chip, h, c], gr.at[chip, h, c])
        for part, first, many in ((pa, 0, ca), (pb, ca, fb - ca)):
            def col(c, _, part=part, first=first):
                to = pl.multiple_of(c * 2 * BLOCK, 2 * BLOCK)
                slots = []
                for r in range(n_model):
                    at = r * fb + c + first
                    slots.append(tabs[at // LANES, 0, at % LANES])
                weight = jnp.concatenate(
                    [jnp.concatenate([gw[i], uw[i]], axis=1) for i in slots], axis=0)
                y = jnp.dot(gat[chip, h].reshape(tall, n_model * BLOCK), weight,
                            preferred_element_type=F32)
                part[j, :, :, :, pl.ds(to, 2 * BLOCK)] = y.astype(BF16).reshape(
                    n_hi, n_lo, rp, 2 * BLOCK)
                return 0

            lax.fori_loop(0, many, col, 0, unroll=True)
            if part is pa:
                for d in range(1, n_lo):
                    l2 = (lo + d) % n_lo
                    send(pa.at[j, :, l2], r1a.at[j, d - 1], s1as.at[j, d - 1],
                         s1ar.at[j, d - 1], (gx, hi * n_lo + l2))
            else:
                for d in range(1, n_hi):
                    h2 = (hi + d) % n_hi
                    send(pb.at[j, h2], r1b.at[j, d - 1], s1bs.at[j, d - 1],
                         s1br.at[j, d - 1], (gx, h2 * n_lo + lo))

    def reduce(job):
        j = number[job]
        for d in range(1, n_lo):
            arrived(r1a.at[j, d - 1], s1ar.at[j, d - 1])
        for e in list(range(1, n_hi)) + [0]:
            h2 = (hi + e) % n_hi
            s = pa[j, h2, lo].astype(F32)
            for d in range(1, n_lo):
                s = s + r1a[j, d - 1, h2].astype(F32)
            if e == 0:
                acca[j] = s
            else:
                s2a[j, e - 1] = s.astype(BF16)
                send(s2a.at[j, e - 1], r2a.at[j, e - 1], s2as.at[j, e - 1],
                     s2ar.at[j, e - 1], (gx, h2 * n_lo + lo))
        for d in range(1, n_hi):
            arrived(r1b.at[j, d - 1], s1br.at[j, d - 1])
        for e in list(range(1, n_lo)) + [0]:
            l2 = (lo + e) % n_lo
            s = pb[j, hi, l2].astype(F32)
            for d in range(1, n_hi):
                s = s + r1b[j, d - 1, l2].astype(F32)
            if e == 0:
                accb[j] = s
            else:
                s2b[j, e - 1] = s.astype(BF16)
                send(s2b.at[j, e - 1], r2b.at[j, e - 1], s2bs.at[j, e - 1],
                     s2br.at[j, e - 1], (gx, hi * n_lo + l2))

    def activate(job):
        j = number[job]
        for d in range(1, n_hi):
            arrived(r2a.at[j, d - 1], s2ar.at[j, d - 1])
        for d in range(1, n_lo):
            arrived(r2b.at[j, d - 1], s2br.at[j, d - 1])
        for c in range(fb):
            acc, got, peers, at = (
                (acca, r2a, n_hi, c) if c < ca else (accb, r2b, n_lo, c - ca))
            cols = pl.ds(at * 2 * BLOCK, 2 * BLOCK)
            s = acc[j, :, cols]
            for d in range(1, peers):
                s = s + got[j, d - 1, :, cols].astype(F32)
            gate, up = s[:, :BLOCK], s[:, BLOCK:]
            hid[c] = (gate / (1.0 + jnp.exp(-gate)) * up).astype(BF16)
        others = [(a, b) for a in range(n_hi) for b in range(n_lo) if a or b]
        others.sort(key=lambda ab: -(ab[0] > 0) - (ab[1] > 0))
        for at, (a, b) in enumerate(others):
            dest = (hi + a) % n_hi * n_lo + (lo + b) % n_lo
            for q in range(used):
                a2s[j, at, :, pl.ds(q * BLOCK, BLOCK)] = hid[kept[0, dest, q]]
            send(a2s.at[j, at], a2r.at[j, gy], xs.at[j, at], xr.at[j, gy], (gx, dest))
        for q in range(used):
            a2r[j, gy, :, pl.ds(q * BLOCK, BLOCK)] = hid[kept[0, gy, q]]

    wide = 2 * BLOCK

    def mix(job):
        j = number[job]
        for d in range(1, n_gy):
            src = (gy + d) % n_gy
            arrived(a2r.at[j, src], xr.at[j, src])

        def col(c, _):
            at = pl.multiple_of(c * wide, wide)
            slots = []
            for r in range(used):
                pair = [r * n_model + c * 2 + i for i in range(2)]
                slots.append([tabs[down_at + p // LANES, 0, p % LANES] for p in pair])
            weight = jnp.concatenate(
                [jnp.concatenate([dw[i] for i in pair], axis=1) for pair in slots], axis=0)
            ps[j, :, pl.ds(at, wide)] = jnp.dot(
                a2r[j].reshape(tall, used * BLOCK), weight,
                preferred_element_type=F32).astype(BF16)
            return 0

        lax.fori_loop(0, n_model * BLOCK // wide, col, 0, unroll=True)
        for d in range(1, per):
            cj = (mc + d) % per
            send(ps.at[j, pl.ds(pl.multiple_of(cj * hr, hr), hr)], fp.at[j, d - 1],
                 fps.at[j, d - 1], fpr.at[j, d - 1], (zc * per + cj, gy))

    def finish(job):
        j, (k, h) = number[job], job
        s = ps[j, pl.ds(pl.multiple_of(mc * hr, hr), hr)].astype(F32)
        for d in range(1, per):
            arrived(fp.at[j, d - 1], fpr.at[j, d - 1])
            s = s + fp[j, d - 1].astype(F32)
        if k:
            f2[j] = s.astype(BF16)
            send(f2.at[j], fr.at[j], fs.at[j], fq.at[j], ((zc ^ k) * per + mc, gy))
        else:
            facc[h] = s

    def total(h):
        s = facc[h]
        for k in range(1, nc):
            j = number[k, h]
            arrived(fr.at[j], fq.at[j])
            s = s + fr[j].astype(F32)
        out[pl.ds(h * hr, hr)] = s.astype(BF16)

    def run(stage, *args):
        with jax.named_scope(f"{stage.__name__}#j={args}"):
            stage(*args)

    for h in range(halves):
        share(zc, h, True, True)
    tables.wait()
    with jax.named_scope("loads"):
        loads[0].wait()
        loads[1].wait()

    far = [(k, h) for k in range(1, nc) for h in range(halves)]
    far = far[:1] + [job for job in far if job[0] > 1] + [job for job in far[1:] if job[0] == 1]
    hops = [(d, h) for d in range(1, nc) for h in range(halves)]

    def need(i):
        if i < len(far):
            k, h = far[i]
            while hops and hops[0] <= (k, h):
                run(relay, *hops.pop(0))

    own = [(0, h) for h in range(halves)]
    n = len(far)
    for job in own:
        run(project, job)
    need(0)
    for i in range(n + 1):
        if i < n:
            run(project, far[i])
            need(i + 1)
        if i == 0:
            run(reduce, own[0])
            loads[2].wait()
        for lag, stage in ((1, reduce), (2, activate), (3, mix), (4, finish)):
            if 0 <= i - lag < n:
                run(stage, far[i - lag])
            if i == n and stage is activate:
                for job in own[1:]:
                    run(reduce, job)
    run(activate, far[n - 1])
    for job in own:
        run(activate, job)
    for lag in (2, 1):
        if n >= lag:
            run(mix, far[n - lag])
            if n > lag:
                run(finish, far[n - lag - 1])
    run(mix, own[0])
    run(finish, far[n - 1])
    for job in own[1:]:
        run(mix, job)
    for job in own:
        run(finish, job)
    for h in range(halves):
        run(total, h)
    for copy, when in sends:
        if when is None:
            copy.wait_send()
        else:
            pl.when(when)(copy.wait_send)


def solution(mesh):
    n_gx, n_gy = mesh.shape["gx"], mesh.shape["gy"]
    n_hi, n_lo = factor(n_gy)
    per = 2 if n_gx % 2 == 0 else 1
    nc = n_gx // per
    halves = 2

    def body(tokens, gate_blocks, up_blocks, gate_coords, gate_count,
             down_blocks, down_rows, down_coords, down_count):
        rows, width = tokens.shape
        n_model = width // BLOCK
        fb = FF // (BLOCK * n_gx)
        ca = (fb + 1) // 2
        cb = fb - ca
        cap, capd, used = gate_blocks.shape[2], down_blocks.shape[2], down_rows.shape[-1]
        hr = rows // halves
        rp = per * hr // n_gy
        jobs = nc * halves
        cfg = (n_gx, n_gy, n_hi, n_lo, per, nc, halves, rp, hr, n_model, fb, ca,
               cap, used, capd)
        wa, wb = ca * 2 * BLOCK, cb * 2 * BLOCK
        kl, kh, kg = max(n_lo - 1, 1), max(n_hi - 1, 1), max(n_gy - 1, 1)
        kp = max(per - 1, 1)
        tabs = -(-n_model * fb // LANES) + -(-used * n_model // LANES)
        vm, sm, dma = pltpu.VMEM, pltpu.SMEM, pltpu.SemaphoreType.DMA
        hbm = pl.BlockSpec(memory_space=pltpu.HBM)
        return pl.pallas_call(
            functools.partial(kernel, cfg),
            out_shape=jax.ShapeDtypeStruct((rows, width), BF16),
            in_specs=[hbm] * 9,
            out_specs=pl.BlockSpec(memory_space=pltpu.VMEM),
            scratch_shapes=[
                sm((2, cap), I32),
                sm((1, 1), I32),
                sm((2, capd), I32),
                sm((1, 1), I32),
                sm(down_rows.shape, I32),
                vm((tabs, 1, LANES), I32),
                sm((tabs, 1, LANES), I32),
                vm((cap + 1, BLOCK, BLOCK), BF16),
                vm((cap + 1, BLOCK, BLOCK), BF16),
                vm((capd + 1, BLOCK, BLOCK), BF16),
                vm((nc, halves, per, hr, width), BF16),
                vm((jobs, n_hi, n_lo, rp, wa), BF16),
                vm((jobs, n_hi, n_lo, rp, wb), BF16),
                vm((jobs, kl, n_hi, rp, wa), BF16),
                vm((jobs, kh, n_lo, rp, wb), BF16),
                vm((jobs, kh, rp, wa), BF16),
                vm((jobs, kl, rp, wb), BF16),
                vm((jobs, kh, rp, wa), BF16),
                vm((jobs, kl, rp, wb), BF16),
                vm((jobs, rp, wa), F32),
                vm((jobs, rp, wb), F32),
                vm((fb, rp, BLOCK), BF16),
                vm((jobs, kg, rp, used * BLOCK), BF16),
                vm((jobs, n_gy, rp, used * BLOCK), BF16),
                vm((jobs, per * hr, width), BF16),
                vm((jobs, kp, hr, width), BF16),
                vm((jobs, hr, width), BF16),
                vm((jobs, hr, width), BF16),
                vm((halves, hr, width), F32),
                dma((8 + halves,)),
                dma((nc, halves, 1 + per)), dma((nc, halves, per)),
                dma((jobs, kl)), dma((jobs, kl)),
                dma((jobs, kh)), dma((jobs, kh)),
                dma((jobs, kh)), dma((jobs, kh)),
                dma((jobs, kl)), dma((jobs, kl)),
                dma((jobs, kg)), dma((jobs, n_gy)),
                dma((jobs,)), dma((jobs,)),
                dma((jobs, kp)), dma((jobs, kp)),
            ],
            compiler_params=pltpu.CompilerParams(
                collective_id=0, has_side_effects=True, vmem_limit_bytes=60 * 1024 * 1024),
        )(gate_coords[0, 0].T, gate_count, down_coords[0, 0].T, down_count, down_rows,
          tokens, gate_blocks.reshape(cap, BLOCK, BLOCK),
          up_blocks.reshape(cap, BLOCK, BLOCK), down_blocks.reshape(capd, BLOCK, BLOCK))

    return jax.shard_map(
        body,
        mesh=mesh,
        in_specs=(
            P("gx", "gy"),
            P("gy", "gx", None, None, None),
            P("gy", "gx", None, None, None),
            P("gy", "gx", None, None),
            P("gy", "gx"),
            P("gx", "gy", None, None, None),
            P("gx", None, None),
            P("gx", "gy", None, None),
            P("gx", "gy"),
        ),
        out_specs=P("gx", "gy"),
        check_vma=False,
    )
```

time: 69.8 us -> 60.7 us (0.87); the launches traced: 68.7 us -> 60.5 us
  Pallas kernels: 63.1 us -> 57.7 us
  other arithmetic: 2.75 us -> 0 us
    pallas_call x1, Pallas kernels: 63.1 us -> 57.7 us  [body(): pl.pallas_call(functools.partial(kernel, cfg), out_shape=jax.ShapeDtypeSt...]
    eq x2 -> x0, other arithmetic: 1.52 us -> none  [inverse(): hit = (place[:, None] == spot[None, :]) & (slot < count)[:, None]]
    reduce_min x2 -> x0, other arithmetic: 1.22 us -> none  [inverse(): return jnp.min(jnp.where(hit, slot[:, None], slots), axis=0)]
where the time goes in v1:
time: 60.7 us; the launch traced here: 60.5 us
  Pallas kernels  57.7 us (95%)
  local copies, waits for them, and re-layouts  1.57 us (3%)
  between operations  1.3 us (2%)
    pallas_call x1, Pallas kernels, body(): pl.pallas_call(functools.partial(kernel, cfg), out_shape=jax.ShapeDtypeSt...  57.7 us
    unnamed x1, local copies, waits for them, and re-layouts  1.57 us

profile of v1, /device:TPU:0, one launch (start us, length us, event | category | flops | bytes accessed | tf_op | source)
XLA Modules:
  0.0 60.5 jit_solution(4910981072781947069)
XLA Ops:
  1.3 57.7 %shard_map.91 = bf16[64,1024]{1,0:T(8,128)(2,1)} custom-call(s32[2,84]{1,0:T(2,128)} %bitcast.12, s32[1,1]{1,0:T(1,128)S(6)} %copy.11.gct_h, s32[2,48]{1,0:T(2,128)} %bitcast.13, s32[1,1]{1,0:T(1,128)S(6)} %copy.12.dct_h, s32[1,4,8]{2,1,0:T(4,128)} %kept_h.1, bf16[64,1024]{1,0:T(8,128)(2,1)} %tok.1, bf16[84,128,128]{2,1,0:T(8,128)(2,1)} %bitcast.9, ...), custom_call_target="tpu_custom_call" | custom-call | tf_op jit(solution)/shard_map/pallas_call | solution.py:372
  59.0 1.6 %copy.13 = bf16[64,1024]{1,0:T(8,128)(2,1)} copy(bf16[64,1024]{1,0:T(8,128)(2,1)} %shard_map.91) | data formatting | bytes 262144

commit v2 on v1

--- a/solution.py
+++ b/solution.py
@@ -9,6 +9,8 @@
 
 BLOCK = 128
 LANES = 128
+LOADS = 1
+EARLY = 1
 FF = 14336
 MESH = pl.DeviceIdType.MESH
 F32, BF16, I32 = jnp.float32, jnp.bfloat16, jnp.int32
@@ -25,7 +27,7 @@
            gco, gct, dco, dct, kept, tabv, tabs,
            gw, uw, dw, gat, pa, pb,
            r1a, r1b, s2a, s2b, r2a, r2b, acca, accb, hid, a2s, a2r, ps, fp, f2, fr, facc,
-           lsem, gs, gr, s1as, s1ar, s1bs, s1br, s2as, s2ar, s2bs, s2br, xs, xr, fs, fq, fps, fpr):
+           lsem, wsem, gs, gr, s1as, s1ar, s1bs, s1br, s2as, s2ar, s2bs, s2br, xs, xr, fs, fq, fps, fpr):
     (n_gx, n_gy, n_hi, n_lo, per, nc, halves, rp, hr, n_model, fb, ca,
      cap, used, capd) = cfg
     gx, gy = lax.axis_index("gx"), lax.axis_index("gy")
@@ -65,11 +67,12 @@
         pltpu.make_async_copy(tok.at[pl.ds(h * hr, hr)], gat.at[zc, h, mc], lsem.at[8 + h])
         for h in range(halves)
     ]
-    loads = [
-        pltpu.make_async_copy(gblk, gw.at[pl.ds(0, cap)], lsem.at[5]),
-        pltpu.make_async_copy(ublk, uw.at[pl.ds(0, cap)], lsem.at[6]),
-        pltpu.make_async_copy(dblk, dw.at[pl.ds(0, capd)], lsem.at[7]),
-    ]
+    loads, last = [], pltpu.make_async_copy(dblk, dw.at[pl.ds(0, capd)], lsem.at[7])
+    size = -(-cap // LOADS)
+    for a in range(0, cap, size):
+        part = pl.ds(a, min(size, cap - a))
+        for i, (src, dst) in enumerate(((gblk, gw), (ublk, uw))):
+            loads.append(pltpu.make_async_copy(src.at[part], dst.at[part], wsem.at[i, a // size]))
     for load in smalls + mine + loads:
         load.start()
 
@@ -122,68 +125,96 @@
                 src_ref=ref, dst_ref=ref, send_sem=sem, recv_sem=sem,
                 device_id=(gx, (gy + 1) % n_gy), device_id_type=MESH).wait_recv()
 
-    def share(c, h, up, down, there=None):
-        def both(a, b):
-            return b if a is None else a & b
+    near = 1 - 2 * (zc % 2)
+
+    def share(c, h, ways, there=None):
         ref = gat.at[c, h, mc]
-        if up:
-            send(ref, ref, gs.at[c, h, 0], gr.at[c, h, mc], ((zc + 1) * per + mc, gy),
-                 both(there, zc < nc - 1))
-        if down:
-            send(ref, ref, gs.at[c, h, 1], gr.at[c, h, mc], ((zc - 1) * per + mc, gy),
-                 both(there, zc > 0))
+        for at, way in enumerate(ways):
+            to = zc + way
+            fits = (to >= 0) & (to < nc)
+            send(ref, ref, gs.at[c, h, at], gr.at[c, h, mc], (to * per + mc, gy),
+                 fits if there is None else there & fits)
         for j in range(1, per):
             send(ref, ref, gs.at[c, h, 1 + j], gr.at[c, h, mc],
                  (zc * per + (mc + j) % per, gy), there)
 
-    def relay(d, h):
-        for c, there, up in ((zc - d, zc >= d, True), (zc + d, zc < nc - d, False)):
-            @pl.when(there)
-            def _(c=c):
-                arrived(gat.at[c, h, mc], gr.at[c, h, mc])
-
-            share(c, h, up, not up, there)
-
-    jobs = [(k, h) for k in range(nc) for h in range(halves)]
-    number = {job: i for i, job in enumerate(jobs)}
-
-    def project(job):
-        j, (k, h) = number[job], job
-        chip = zc ^ k
-        for d in range(1, per):
-            c = (mc + d) % per
-            arrived(gat.at[chip, h, c], gr.at[chip, h, c])
-        for part, first, many in ((pa, 0, ca), (pb, ca, fb - ca)):
-            def col(c, _, part=part, first=first):
-                to = pl.multiple_of(c * 2 * BLOCK, 2 * BLOCK)
-                slots = []
-                for r in range(n_model):
-                    at = r * fb + c + first
-                    slots.append(tabs[at // LANES, 0, at % LANES])
-                weight = jnp.concatenate(
-                    [jnp.concatenate([gw[i], uw[i]], axis=1) for i in slots], axis=0)
-                y = jnp.dot(gat[chip, h].reshape(tall, n_model * BLOCK), weight,
-                            preferred_element_type=F32)
-                part[j, :, :, :, pl.ds(to, 2 * BLOCK)] = y.astype(BF16).reshape(
-                    n_hi, n_lo, rp, 2 * BLOCK)
-                return 0
-
-            lax.fori_loop(0, many, col, 0, unroll=True)
-            if part is pa:
-                for d in range(1, n_lo):
-                    l2 = (lo + d) % n_lo
-                    send(pa.at[j, :, l2], r1a.at[j, d - 1], s1as.at[j, d - 1],
-                         s1ar.at[j, d - 1], (gx, hi * n_lo + l2))
-            else:
-                for d in range(1, n_hi):
-                    h2 = (hi + d) % n_hi
-                    send(pb.at[j, h2], r1b.at[j, d - 1], s1bs.at[j, d - 1],
-                         s1br.at[j, d - 1], (gx, h2 * n_lo + lo))
+    def relay(d, h, way):
+        c = zc + way * d
+        there = (c >= 0) & (c < nc)
+
+        @pl.when(there)
+        def _():
+            arrived(gat.at[c, h, mc], gr.at[c, h, mc])
+
+        share(c, h, (-way,), there)
+
+    own = [(h, zc, h) for h in range(halves)]
+    plain = [(k, h) for k in range(1, nc) for h in range(halves)]
+    late = plain[:1] + [kh for kh in plain if kh[0] > 1] + plain[1:halves]
+    turn = zc % 2 * jnp.minimum(nc - 1 - zc, 1)
+    far = []
+    for i, (a, b) in enumerate(zip(late, plain)):
+        k, h = (u + turn * (v - u) if u != v else u for u, v in zip(a, b))
+        far.append((halves + i, zc ^ k, h))
+
+    def spans(many, pieces):
+        size = -(-many // pieces)
+        return [(a, min(a + size, many)) for a in range(0, many, size)]
+
+    def project(first_job, count=1, pieces=1):
+        j, chip, h = first_job
+        for g in [h + i for i in range(count)]:
+            for d in range(1, per):
+                c = (mc + d) % per
+                arrived(gat.at[chip, g, c], gr.at[chip, g, c])
+        parts = ((pa, 0, spans(ca, pieces)), (pb, ca, spans(fb - ca, pieces)))
+        for piece in range(pieces):
+            for part, first, cuts in parts:
+                lo_c, hi_c = cuts[piece]
+
+                def col(i, _, part=part, first=first, lo_c=lo_c):
+                    c = i + lo_c
+                    to = pl.multiple_of(c * 2 * BLOCK, 2 * BLOCK)
+                    slots = []
+                    for r in range(n_model):
+                        at = r * fb + c + first
+                        slots.append(tabs[at // LANES, 0, at % LANES])
+                    weight = jnp.concatenate(
+                        [jnp.concatenate([gw[i], uw[i]], axis=1) for i in slots], axis=0)
+                    x = gat[chip, pl.ds(h, count)].reshape(count * tall, n_model * BLOCK)
+                    y = jnp.dot(x, weight, preferred_element_type=F32)
+                    part[pl.ds(j, count), :, :, :, pl.ds(to, 2 * BLOCK)] = y.astype(
+                        BF16).reshape(count, n_hi, n_lo, rp, 2 * BLOCK)
+                    return 0
+
+                lax.fori_loop(0, hi_c - lo_c, col, 0, unroll=True)
+                cols = pl.ds(lo_c * 2 * BLOCK, (hi_c - lo_c) * 2 * BLOCK)
+                for g in range(j, j + count):
+                    split[g] = pieces
+                    if part is pa:
+                        for d in range(1, n_lo):
+                            l2 = (lo + d) % n_lo
+                            send(pa.at[g, :, l2, :, cols], r1a.at[g, d - 1, :, :, cols],
+                                 s1as.at[g, d - 1, piece], s1ar.at[g, d - 1, piece],
+                                 (gx, hi * n_lo + l2))
+                    else:
+                        for d in range(1, n_hi):
+                            h2 = (hi + d) % n_hi
+                            send(pb.at[g, h2, :, :, cols], r1b.at[g, d - 1, :, :, cols],
+                                 s1bs.at[g, d - 1, piece], s1br.at[g, d - 1, piece],
+                                 (gx, h2 * n_lo + lo))
+
+    split = {}
+
+    def first_arrived(ref, sem, many, pieces):
+        for piece, (a, b) in enumerate(spans(many, pieces)):
+            cols = pl.ds(a * 2 * BLOCK, (b - a) * 2 * BLOCK)
+            arrived(ref.at[:, :, cols], sem.at[piece])
 
     def reduce(job):
-        j = number[job]
+        j = job[0]
         for d in range(1, n_lo):
-            arrived(r1a.at[j, d - 1], s1ar.at[j, d - 1])
+            first_arrived(r1a.at[j, d - 1], s1ar.at[j, d - 1], ca, split[j])
         for e in list(range(1, n_hi)) + [0]:
             h2 = (hi + e) % n_hi
             s = pa[j, h2, lo].astype(F32)
@@ -196,7 +227,7 @@
                 send(s2a.at[j, e - 1], r2a.at[j, e - 1], s2as.at[j, e - 1],
                      s2ar.at[j, e - 1], (gx, h2 * n_lo + lo))
         for d in range(1, n_hi):
-            arrived(r1b.at[j, d - 1], s1br.at[j, d - 1])
+            first_arrived(r1b.at[j, d - 1], s1br.at[j, d - 1], fb - ca, split[j])
         for e in list(range(1, n_lo)) + [0]:
             l2 = (lo + e) % n_lo
             s = pb[j, hi, l2].astype(F32)
@@ -210,7 +241,7 @@
                      s2br.at[j, e - 1], (gx, hi * n_lo + l2))
 
     def activate(job):
-        j = number[job]
+        j = job[0]
         for d in range(1, n_hi):
             arrived(r2a.at[j, d - 1], s2ar.at[j, d - 1])
         for d in range(1, n_lo):
@@ -237,7 +268,7 @@
     wide = 2 * BLOCK
 
     def mix(job):
-        j = number[job]
+        j = job[0]
         for d in range(1, n_gy):
             src = (gy + d) % n_gy
             arrived(a2r.at[j, src], xr.at[j, src])
@@ -262,74 +293,82 @@
                  fps.at[j, d - 1], fpr.at[j, d - 1], (zc * per + cj, gy))
 
     def finish(job):
-        j, (k, h) = number[job], job
+        j, chip, h = job
         s = ps[j, pl.ds(pl.multiple_of(mc * hr, hr), hr)].astype(F32)
         for d in range(1, per):
             arrived(fp.at[j, d - 1], fpr.at[j, d - 1])
             s = s + fp[j, d - 1].astype(F32)
-        if k:
+        if j < halves:
+            facc[j] = s
+        else:
             f2[j] = s.astype(BF16)
-            send(f2.at[j], fr.at[j], fs.at[j], fq.at[j], ((zc ^ k) * per + mc, gy))
-        else:
-            facc[h] = s
+            send(f2.at[j], fr.at[zc, h], fs.at[j], fq.at[zc, h], (chip * per + mc, gy))
 
     def total(h):
         s = facc[h]
         for k in range(1, nc):
-            j = number[k, h]
-            arrived(fr.at[j], fq.at[j])
-            s = s + fr[j].astype(F32)
+            c = zc ^ k
+            arrived(fr.at[c, h], fq.at[c, h])
+            s = s + fr[c, h].astype(F32)
         out[pl.ds(h * hr, hr)] = s.astype(BF16)
 
     def run(stage, *args):
-        with jax.named_scope(f"{stage.__name__}#j={args}"):
+        tag = args[0][0] if isinstance(args[0], tuple) else args[0]
+        with jax.named_scope(f"{stage.__name__}#j={tag}"):
             stage(*args)
 
     for h in range(halves):
-        share(zc, h, True, True)
+        share(zc, h, (1, -1))
     tables.wait()
     with jax.named_scope("loads"):
-        loads[0].wait()
-        loads[1].wait()
-
-    far = [(k, h) for k in range(1, nc) for h in range(halves)]
-    far = far[:1] + [job for job in far if job[0] > 1] + [job for job in far[1:] if job[0] == 1]
-    hops = [(d, h) for d in range(1, nc) for h in range(halves)]
+        for load in loads:
+            load.wait()
+    last.start()
+
+    hops = [(d, h, w) for d in range(1, nc) for h in range(halves) for w in (1, -1)]
 
     def need(i):
         if i < len(far):
-            k, h = far[i]
-            while hops and hops[0] <= (k, h):
-                run(relay, *hops.pop(0))
-
-    own = [(0, h) for h in range(halves)]
+            reach = (1, 0) if i == 0 else max(late[i], plain[i])
+            while hops and hops[0][:2] <= reach:
+                d, h, w = hops.pop(0)
+                run(relay, d, h, near * w)
+
     n = len(far)
-    for job in own:
-        run(project, job)
+
+    def step(stage, i):
+        if 0 <= i < n:
+            run(stage, far[i])
+
+    run(project, own[0], halves, 2)
     need(0)
     for i in range(n + 1):
-        if i < n:
-            run(project, far[i])
-            need(i + 1)
+        step(project, i)
         if i == 0:
-            run(reduce, own[0])
-            loads[2].wait()
-        for lag, stage in ((1, reduce), (2, activate), (3, mix), (4, finish)):
-            if 0 <= i - lag < n:
-                run(stage, far[i - lag])
-            if i == n and stage is activate:
-                for job in own[1:]:
-                    run(reduce, job)
-    run(activate, far[n - 1])
-    for job in own:
+            last.wait()
+            while hops and hops[0][0] == 1:
+                d, h, w = hops.pop(0)
+                run(relay, d, h, near * w)
+            for job in own[:EARLY]:
+                run(reduce, job)
+        step(finish, i - 4)
+        step(reduce, i - 1)
+        step(activate, i - 2)
+        if i == n:
+            for job in own[EARLY:]:
+                run(reduce, job)
+        step(mix, i - 3)
+        need(i + 1)
+    step(activate, n - 1)
+    run(activate, own[0])
+    step(finish, n - 3)
+    step(mix, n - 2)
+    for job in own[1:]:
         run(activate, job)
-    for lag in (2, 1):
-        if n >= lag:
-            run(mix, far[n - lag])
-            if n > lag:
-                run(finish, far[n - lag - 1])
+    step(finish, n - 2)
+    step(mix, n - 1)
     run(mix, own[0])
-    run(finish, far[n - 1])
+    step(finish, n - 1)
     for job in own[1:]:
         run(mix, job)
     for job in own:
@@ -371,7 +410,7 @@
         hbm = pl.BlockSpec(memory_space=pltpu.HBM)
         return pl.pallas_call(
             functools.partial(kernel, cfg),
-            out_shape=jax.ShapeDtypeStruct((rows, width), BF16),
+            out_shape=pltpu.VMEM((rows, width), BF16),
             in_specs=[hbm] * 9,
             out_specs=pl.BlockSpec(memory_space=pltpu.VMEM),
             scratch_shapes=[
@@ -402,16 +441,16 @@
                 vm((jobs, per * hr, width), BF16),
                 vm((jobs, kp, hr, width), BF16),
                 vm((jobs, hr, width), BF16),
-                vm((jobs, hr, width), BF16),
+                vm((nc, halves, hr, width), BF16),
                 vm((halves, hr, width), F32),
-                dma((8 + halves,)),
+                dma((8 + halves,)), dma((2, LOADS)),
                 dma((nc, halves, 1 + per)), dma((nc, halves, per)),
-                dma((jobs, kl)), dma((jobs, kl)),
-                dma((jobs, kh)), dma((jobs, kh)),
+                dma((jobs, kl, 2)), dma((jobs, kl, 2)),
+                dma((jobs, kh, 2)), dma((jobs, kh, 2)),
                 dma((jobs, kh)), dma((jobs, kh)),
                 dma((jobs, kl)), dma((jobs, kl)),
                 dma((jobs, kg)), dma((jobs, n_gy)),
-                dma((jobs,)), dma((jobs,)),
+                dma((jobs,)), dma((nc, halves)),
                 dma((jobs, kp)), dma((jobs, kp)),
             ],
             compiler_params=pltpu.CompilerParams(

time: 60.7 us -> 56.5 us (0.931)
  Pallas kernels: 57.7 us -> 54.3 us
  local copies, waits for them, and re-layouts: 1.57 us -> 0.66 us
    pallas_call x1, Pallas kernels: 57.7 us -> 54.3 us  [body(): pl.pallas_call(functools.partial(kernel, cfg), out_shape=pltpu.VMEM((rows...]
    unnamed x1, local copies, waits for them, and re-layouts: 1.57 us -> 0.66 us
where the time goes in v2:
time: 56.5 us; the launch traced here: 56.3 us
  Pallas kernels  54.3 us (96%)
  between operations  1.3 us (2%)
  local copies, waits for them, and re-layouts  0.66 us (1%)
    pallas_call x1, Pallas kernels, body(): pl.pallas_call(functools.partial(kernel, cfg), out_shape=pltpu.VMEM((rows...  54.3 us

profile of v2, /device:TPU:0, one launch (start us, length us, event | category | flops | bytes accessed | tf_op | source)
XLA Modules:
  0.0 56.3 jit_solution(6802177424736197635)
XLA Ops:
  1.3 54.3 %shard_map.91 = bf16[64,1024]{1,0:T(8,128)(2,1)S(1)} custom-call(s32[2,84]{1,0:T(2,128)} %bitcast.12, s32[1,1]{1,0:T(1,128)S(6)} %copy.12.gct_h, s32[2,48]{1,0:T(2,128)} %bitcast.13, s32[1,1]{1,0:T(1,128)S(6)} %copy.13.dct_h, s32[1,4,8]{2,1,0:T(4,128)} %kept_h.1, bf16[64,1024]{1,0:T(8,128)(2,1)} %tok.1, bf16[84,128,128]{2,1,0:T(8,128)(2,1)} %bitcast.9, ...), custom_call_target="tpu_custom_call" | custom-call | tf_op jit(solution)/shard_map/pallas_call | solution.py:411
  55.6 0.7 %copy.11 = bf16[64,1024]{1,0:T(8,128)(2,1)} copy(bf16[64,1024]{1,0:T(8,128)(2,1)S(1)} %shard_map.91) | data formatting | bytes 262144

commit v3 on v2

--- a/solution.py
+++ b/solution.py
@@ -9,7 +9,6 @@
 
 BLOCK = 128
 LANES = 128
-LOADS = 1
 EARLY = 1
 FF = 14336
 MESH = pl.DeviceIdType.MESH
@@ -27,7 +26,7 @@
            gco, gct, dco, dct, kept, tabv, tabs,
            gw, uw, dw, gat, pa, pb,
            r1a, r1b, s2a, s2b, r2a, r2b, acca, accb, hid, a2s, a2r, ps, fp, f2, fr, facc,
-           lsem, wsem, gs, gr, s1as, s1ar, s1bs, s1br, s2as, s2ar, s2bs, s2br, xs, xr, fs, fq, fps, fpr):
+           lsem, gs, gr, s1as, s1ar, s1bs, s1br, s2as, s2ar, s2bs, s2br, xs, xr, fs, fq, fps, fpr):
     (n_gx, n_gy, n_hi, n_lo, per, nc, halves, rp, hr, n_model, fb, ca,
      cap, used, capd) = cfg
     gx, gy = lax.axis_index("gx"), lax.axis_index("gy")
@@ -67,13 +66,12 @@
         pltpu.make_async_copy(tok.at[pl.ds(h * hr, hr)], gat.at[zc, h, mc], lsem.at[8 + h])
         for h in range(halves)
     ]
-    loads, last = [], pltpu.make_async_copy(dblk, dw.at[pl.ds(0, capd)], lsem.at[7])
-    size = -(-cap // LOADS)
-    for a in range(0, cap, size):
-        part = pl.ds(a, min(size, cap - a))
-        for i, (src, dst) in enumerate(((gblk, gw), (ublk, uw))):
-            loads.append(pltpu.make_async_copy(src.at[part], dst.at[part], wsem.at[i, a // size]))
-    for load in smalls + mine + loads:
+    loads = [
+        pltpu.make_async_copy(gblk, gw.at[pl.ds(0, cap)], lsem.at[5]),
+        pltpu.make_async_copy(ublk, uw.at[pl.ds(0, cap)], lsem.at[6]),
+        pltpu.make_async_copy(dblk, dw.at[pl.ds(0, capd)], lsem.at[7]),
+    ]
+    for load in smalls + mine + loads[:1]:
         load.start()
 
     def table(coords, count, slots, inner, spots, first):
@@ -99,6 +97,7 @@
         dw[capd] = jnp.zeros((BLOCK, BLOCK), BF16)
         tables = pltpu.make_async_copy(tabv, tabs, lsem.at[0])
         tables.start()
+        loads[1].start()
         for load in mine:
             load.wait()
 
@@ -158,37 +157,35 @@
         far.append((halves + i, zc ^ k, h))
 
     def spans(many, pieces):
-        size = -(-many // pieces)
-        return [(a, min(a + size, many)) for a in range(0, many, size)]
-
-    def project(first_job, count=1, pieces=1):
+        cut = many // 2
+        return [(0, cut), (cut, many)] if pieces == 2 and cut else [(0, many)]
+
+    def project(first_job, count=1, pieces=1, between=None):
         j, chip, h = first_job
         for g in [h + i for i in range(count)]:
             for d in range(1, per):
                 c = (mc + d) % per
                 arrived(gat.at[chip, g, c], gr.at[chip, g, c])
-        parts = ((pa, 0, spans(ca, pieces)), (pb, ca, spans(fb - ca, pieces)))
+        parts = ((pa, 0, ca), (pb, ca, fb - ca))
         for piece in range(pieces):
-            for part, first, cuts in parts:
-                lo_c, hi_c = cuts[piece]
-
-                def col(i, _, part=part, first=first, lo_c=lo_c):
-                    c = i + lo_c
-                    to = pl.multiple_of(c * 2 * BLOCK, 2 * BLOCK)
-                    slots = []
-                    for r in range(n_model):
-                        at = r * fb + c + first
-                        slots.append(tabs[at // LANES, 0, at % LANES])
-                    weight = jnp.concatenate(
-                        [jnp.concatenate([gw[i], uw[i]], axis=1) for i in slots], axis=0)
+            for part, first, many in parts:
+                cuts = spans(many, pieces)
+                if piece >= len(cuts):
+                    continue
+                start, stop = cuts[piece]
+                for t in range(start, stop):
+                    columns = []
+                    for b in (2 * t, 2 * t + 1):
+                        ref, c = (gw, b) if b < many else (uw, b - many)
+                        at = [r * fb + c + first for r in range(n_model)]
+                        columns.append(jnp.concatenate(
+                            [ref[tabs[a // LANES, 0, a % LANES]] for a in at], axis=0))
                     x = gat[chip, pl.ds(h, count)].reshape(count * tall, n_model * BLOCK)
-                    y = jnp.dot(x, weight, preferred_element_type=F32)
-                    part[pl.ds(j, count), :, :, :, pl.ds(to, 2 * BLOCK)] = y.astype(
-                        BF16).reshape(count, n_hi, n_lo, rp, 2 * BLOCK)
-                    return 0
-
-                lax.fori_loop(0, hi_c - lo_c, col, 0, unroll=True)
-                cols = pl.ds(lo_c * 2 * BLOCK, (hi_c - lo_c) * 2 * BLOCK)
+                    y = jnp.dot(x, jnp.concatenate(columns, axis=1),
+                                preferred_element_type=F32)
+                    part[pl.ds(j, count), :, :, :, pl.ds(t * 2 * BLOCK, 2 * BLOCK)] = (
+                        y.astype(BF16).reshape(count, n_hi, n_lo, rp, 2 * BLOCK))
+                cols = pl.ds(start * 2 * BLOCK, (stop - start) * 2 * BLOCK)
                 for g in range(j, j + count):
                     split[g] = pieces
                     if part is pa:
@@ -203,6 +200,8 @@
                             send(pb.at[g, h2, :, :, cols], r1b.at[g, d - 1, :, :, cols],
                                  s1bs.at[g, d - 1, piece], s1br.at[g, d - 1, piece],
                                  (gx, h2 * n_lo + lo))
+            if between is not None and piece == 0:
+                between()
 
     split = {}
 
@@ -247,13 +246,16 @@
         for d in range(1, n_lo):
             arrived(r2b.at[j, d - 1], s2br.at[j, d - 1])
         for c in range(fb):
-            acc, got, peers, at = (
-                (acca, r2a, n_hi, c) if c < ca else (accb, r2b, n_lo, c - ca))
-            cols = pl.ds(at * 2 * BLOCK, 2 * BLOCK)
-            s = acc[j, :, cols]
-            for d in range(1, peers):
-                s = s + got[j, d - 1, :, cols].astype(F32)
-            gate, up = s[:, :BLOCK], s[:, BLOCK:]
+            acc, got, peers, at, many = (
+                (acca, r2a, n_hi, c, ca) if c < ca else (accb, r2b, n_lo, c - ca, fb - ca))
+            both = []
+            for b in (at, many + at):
+                cols = pl.ds(b * BLOCK, BLOCK)
+                v = acc[j, :, cols]
+                for d in range(1, peers):
+                    v = v + got[j, d - 1, :, cols].astype(F32)
+                both.append(v)
+            gate, up = both
             hid[c] = (gate / (1.0 + jnp.exp(-gate)) * up).astype(BF16)
         others = [(a, b) for a in range(n_hi) for b in range(n_lo) if a or b]
         others.sort(key=lambda ab: -(ab[0] > 0) - (ab[1] > 0))
@@ -321,9 +323,7 @@
         share(zc, h, (1, -1))
     tables.wait()
     with jax.named_scope("loads"):
-        for load in loads:
-            load.wait()
-    last.start()
+        loads[0].wait()
 
     hops = [(d, h, w) for d in range(1, nc) for h in range(halves) for w in (1, -1)]
 
@@ -340,12 +340,16 @@
         if 0 <= i < n:
             run(stage, far[i])
 
-    run(project, own[0], halves, 2)
+    def more():
+        loads[1].wait()
+        loads[2].start()
+
+    run(project, own[0], halves, 2, more)
     need(0)
     for i in range(n + 1):
         step(project, i)
         if i == 0:
-            last.wait()
+            loads[2].wait()
             while hops and hops[0][0] == 1:
                 d, h, w = hops.pop(0)
                 run(relay, d, h, near * w)
@@ -443,7 +447,7 @@
                 vm((jobs, hr, width), BF16),
                 vm((nc, halves, hr, width), BF16),
                 vm((halves, hr, width), F32),
-                dma((8 + halves,)), dma((2, LOADS)),
+                dma((8 + halves,)),
                 dma((nc, halves, 1 + per)), dma((nc, halves, per)),
                 dma((jobs, kl, 2)), dma((jobs, kl, 2)),
                 dma((jobs, kh, 2)), dma((jobs, kh, 2)),

time: 56.5 us -> 55 us (0.973)
  Pallas kernels: 54.3 us -> 52.9 us
    pallas_call x1, Pallas kernels: 54.3 us -> 52.9 us  [body(): pl.pallas_call(functools.partial(kernel, cfg), out_shape=pltpu.VMEM((rows...]
where the time goes in v3:
time: 55 us; the launch traced here: 54.8 us
  Pallas kernels  52.9 us (96%)
  between operations  1.3 us (2%)
  local copies, waits for them, and re-layouts  0.66 us (1%)
    pallas_call x1, Pallas kernels, body(): pl.pallas_call(functools.partial(kernel, cfg), out_shape=pltpu.VMEM((rows...  52.9 us

profile of v3, /device:TPU:0, one launch (start us, length us, event | category | flops | bytes accessed | tf_op | source)
XLA Modules:
  0.0 54.8 jit_solution(4159526641538885497)
XLA Ops:
  1.3 52.9 %shard_map.91 = bf16[64,1024]{1,0:T(8,128)(2,1)S(1)} custom-call(s32[2,84]{1,0:T(2,128)} %bitcast.12, s32[1,1]{1,0:T(1,128)S(6)} %copy.12.gct_h, s32[2,48]{1,0:T(2,128)} %bitcast.13, s32[1,1]{1,0:T(1,128)S(6)} %copy.13.dct_h, s32[1,4,8]{2,1,0:T(4,128)} %kept_h.1, bf16[64,1024]{1,0:T(8,128)(2,1)} %tok.1, bf16[84,128,128]{2,1,0:T(8,128)(2,1)} %bitcast.9, ...), custom_call_target="tpu_custom_call" | custom-call | tf_op jit(solution)/shard_map/pallas_call | solution.py:415
  54.2 0.7 %copy.11 = bf16[64,1024]{1,0:T(8,128)(2,1)} copy(bf16[64,1024]{1,0:T(8,128)(2,1)S(1)} %shard_map.91) | data formatting | bytes 262144

commit v4 on v3

--- a/solution.py
+++ b/solution.py
@@ -9,7 +9,7 @@
 
 BLOCK = 128
 LANES = 128
-EARLY = 1
+PIECES = 3
 FF = 14336
 MESH = pl.DeviceIdType.MESH
 F32, BF16, I32 = jnp.float32, jnp.bfloat16, jnp.int32
@@ -124,8 +124,6 @@
                 src_ref=ref, dst_ref=ref, send_sem=sem, recv_sem=sem,
                 device_id=(gx, (gy + 1) % n_gy), device_id_type=MESH).wait_recv()
 
-    near = 1 - 2 * (zc % 2)
-
     def share(c, h, ways, there=None):
         ref = gat.at[c, h, mc]
         for at, way in enumerate(ways):
@@ -150,15 +148,23 @@
     own = [(h, zc, h) for h in range(halves)]
     plain = [(k, h) for k in range(1, nc) for h in range(halves)]
     late = plain[:1] + [kh for kh in plain if kh[0] > 1] + plain[1:halves]
-    turn = zc % 2 * jnp.minimum(nc - 1 - zc, 1)
+    peak = [(k, 0) for k in range(1, nc)] + [
+        (k, h) for k in range(nc - 1, 0, -1) for h in range(1, halves)]
+
+    def order(z):
+        return peak if z == nc - 1 else plain if z % 2 else late
+
+    top = 1 - jnp.minimum(nc - 1 - zc, 1)
+    odd = zc % 2 * (1 - top)
     far = []
-    for i, (a, b) in enumerate(zip(late, plain)):
-        k, h = (u + turn * (v - u) if u != v else u for u, v in zip(a, b))
+    for i, (a, b, c) in enumerate(zip(late, plain, peak)):
+        k, h = (u + odd * (v - u) + top * (w - u) for u, v, w in zip(a, b, c))
         far.append((halves + i, zc ^ k, h))
 
     def spans(many, pieces):
         cut = many // 2
-        return [(0, cut), (cut, many)] if pieces == 2 and cut else [(0, many)]
+        ends = [0, 1, cut, many] if pieces > 1 and cut > 1 else [0, many]
+        return list(zip(ends, ends[1:]))
 
     def project(first_job, count=1, pieces=1, between=None):
         j, chip, h = first_job
@@ -200,7 +206,7 @@
                             send(pb.at[g, h2, :, :, cols], r1b.at[g, d - 1, :, :, cols],
                                  s1bs.at[g, d - 1, piece], s1br.at[g, d - 1, piece],
                                  (gx, h2 * n_lo + lo))
-            if between is not None and piece == 0:
+            if between is not None and piece == max(pieces - 2, 0):
                 between()
 
     split = {}
@@ -325,14 +331,17 @@
     with jax.named_scope("loads"):
         loads[0].wait()
 
-    hops = [(d, h, w) for d in range(1, nc) for h in range(halves) for w in (1, -1)]
+    hops = {w: [(d, h) for d in range(1, nc) for h in range(halves)] for w in (-1, 1)}
 
     def need(i):
-        if i < len(far):
-            reach = (1, 0) if i == 0 else max(late[i], plain[i])
-            while hops and hops[0][:2] <= reach:
-                d, h, w = hops.pop(0)
-                run(relay, d, h, near * w)
+        for w in (-1, 1):
+            reach = [(1, i)] if i < halves else []
+            for z in range(nc if i < len(far) else 0):
+                k, h = order(z)[i]
+                if ((z ^ k) - z) * w > 0:
+                    reach.append((abs((z ^ k) - z), h))
+            while hops[w] and reach and hops[w][0] <= max(reach):
+                run(relay, *hops[w].pop(0), w)
 
     n = len(far)
 
@@ -344,25 +353,25 @@
         loads[1].wait()
         loads[2].start()
 
-    run(project, own[0], halves, 2, more)
+    run(project, own[0], halves, PIECES, more)
     need(0)
     for i in range(n + 1):
         step(project, i)
         if i == 0:
             loads[2].wait()
-            while hops and hops[0][0] == 1:
-                d, h, w = hops.pop(0)
-                run(relay, d, h, near * w)
-            for job in own[:EARLY]:
-                run(reduce, job)
+            for w in (-1, 1):
+                run(relay, *hops[w].pop(0), w)
+            run(reduce, own[0])
+            need(1)
         step(finish, i - 4)
         step(reduce, i - 1)
         step(activate, i - 2)
         if i == n:
-            for job in own[EARLY:]:
+            for job in own[1:]:
                 run(reduce, job)
         step(mix, i - 3)
-        need(i + 1)
+        if i:
+            need(i + 1)
     step(activate, n - 1)
     run(activate, own[0])
     step(finish, n - 3)
@@ -449,8 +458,8 @@
                 vm((halves, hr, width), F32),
                 dma((8 + halves,)),
                 dma((nc, halves, 1 + per)), dma((nc, halves, per)),
-                dma((jobs, kl, 2)), dma((jobs, kl, 2)),
-                dma((jobs, kh, 2)), dma((jobs, kh, 2)),
+                dma((jobs, kl, PIECES)), dma((jobs, kl, PIECES)),
+                dma((jobs, kh, PIECES)), dma((jobs, kh, PIECES)),
                 dma((jobs, kh)), dma((jobs, kh)),
                 dma((jobs, kl)), dma((jobs, kl)),
                 dma((jobs, kg)), dma((jobs, n_gy)),

time: 55 us -> 54.6 us (level)
  no operation moved by 1% of the time
where the time goes in v4:
time: 54.6 us; the launch traced here: 54.3 us
  Pallas kernels  52.4 us (96%)
  between operations  1.3 us (2%)
  local copies, waits for them, and re-layouts  0.66 us (1%)
    pallas_call x1, Pallas kernels, body(): pl.pallas_call(functools.partial(kernel, cfg), out_shape=pltpu.VMEM((rows...  52.4 us

profile of v4, /device:TPU:0, one launch (start us, length us, event | category | flops | bytes accessed | tf_op | source)
XLA Modules:
  0.0 54.3 jit_solution(380660720180471484)
XLA Ops:
  1.3 52.4 %shard_map.91 = bf16[64,1024]{1,0:T(8,128)(2,1)S(1)} custom-call(s32[2,84]{1,0:T(2,128)} %bitcast.12, s32[1,1]{1,0:T(1,128)S(6)} %copy.12.gct_h, s32[2,48]{1,0:T(2,128)} %bitcast.13, s32[1,1]{1,0:T(1,128)S(6)} %copy.13.dct_h, s32[1,4,8]{2,1,0:T(4,128)} %kept_h.1, bf16[64,1024]{1,0:T(8,128)(2,1)} %tok.1, bf16[84,128,128]{2,1,0:T(8,128)(2,1)} %bitcast.9, ...), custom_call_target="tpu_custom_call" | custom-call | tf_op jit(solution)/shard_map/pallas_call | solution.py:424
  53.7 0.7 %copy.11 = bf16[64,1024]{1,0:T(8,128)(2,1)} copy(bf16[64,1024]{1,0:T(8,128)(2,1)S(1)} %shard_map.91) | data formatting | bytes 262144

commit v5 on v4

--- a/solution.py
+++ b/solution.py
@@ -26,7 +26,7 @@
            gco, gct, dco, dct, kept, tabv, tabs,
            gw, uw, dw, gat, pa, pb,
            r1a, r1b, s2a, s2b, r2a, r2b, acca, accb, hid, a2s, a2r, ps, fp, f2, fr, facc,
-           lsem, gs, gr, s1as, s1ar, s1bs, s1br, s2as, s2ar, s2bs, s2br, xs, xr, fs, fq, fps, fpr):
+           lsem, gs, ks, gr, s1as, s1ar, s1bs, s1br, s2as, s2ar, s2bs, s2br, xs, xr, fs, fq, fps, fpr):
     (n_gx, n_gy, n_hi, n_lo, per, nc, halves, rp, hr, n_model, fb, ca,
      cap, used, capd) = cfg
     gx, gy = lax.axis_index("gx"), lax.axis_index("gy")
@@ -108,7 +108,7 @@
 
     sends = []
 
-    def send(src, dst, ssem, rsem, dev, when=None):
+    def send(src, dst, ssem, rsem, dev, when=None, listed=False):
         copy = pltpu.make_async_remote_copy(
             src_ref=src, dst_ref=dst, send_sem=ssem, recv_sem=rsem,
             device_id=dev, device_id_type=MESH)
@@ -116,7 +116,13 @@
             copy.start()
         else:
             pl.when(when)(copy.start)
-        sends.append((copy, when))
+        if listed:
+            sends.append((copy, when))
+
+    def left(ref, sem):
+        pltpu.make_async_remote_copy(
+            src_ref=ref, dst_ref=ref, send_sem=sem, recv_sem=sem,
+            device_id=(gx, (gy + 1) % n_gy), device_id_type=MESH).wait_send()
 
     def arrived(ref, sem):
         with jax.named_scope("w"):
@@ -130,9 +136,9 @@
             to = zc + way
             fits = (to >= 0) & (to < nc)
             send(ref, ref, gs.at[c, h, at], gr.at[c, h, mc], (to * per + mc, gy),
-                 fits if there is None else there & fits)
+                 fits if there is None else there & fits, True)
         for j in range(1, per):
-            send(ref, ref, gs.at[c, h, 1 + j], gr.at[c, h, mc],
+            send(ref, ref, ks.at[j - 1], gr.at[c, h, mc],
                  (zc * per + (mc + j) % per, gy), there)
 
     def relay(d, h, way):
@@ -193,33 +199,25 @@
                         y.astype(BF16).reshape(count, n_hi, n_lo, rp, 2 * BLOCK))
                 cols = pl.ds(start * 2 * BLOCK, (stop - start) * 2 * BLOCK)
                 for g in range(j, j + count):
-                    split[g] = pieces
                     if part is pa:
                         for d in range(1, n_lo):
                             l2 = (lo + d) % n_lo
                             send(pa.at[g, :, l2, :, cols], r1a.at[g, d - 1, :, :, cols],
-                                 s1as.at[g, d - 1, piece], s1ar.at[g, d - 1, piece],
+                                 s1as.at[0], s1ar.at[g],
                                  (gx, hi * n_lo + l2))
                     else:
                         for d in range(1, n_hi):
                             h2 = (hi + d) % n_hi
                             send(pb.at[g, h2, :, :, cols], r1b.at[g, d - 1, :, :, cols],
-                                 s1bs.at[g, d - 1, piece], s1br.at[g, d - 1, piece],
+                                 s1bs.at[0], s1br.at[g],
                                  (gx, h2 * n_lo + lo))
             if between is not None and piece == max(pieces - 2, 0):
                 between()
 
-    split = {}
-
-    def first_arrived(ref, sem, many, pieces):
-        for piece, (a, b) in enumerate(spans(many, pieces)):
-            cols = pl.ds(a * 2 * BLOCK, (b - a) * 2 * BLOCK)
-            arrived(ref.at[:, :, cols], sem.at[piece])
-
     def reduce(job):
         j = job[0]
-        for d in range(1, n_lo):
-            first_arrived(r1a.at[j, d - 1], s1ar.at[j, d - 1], ca, split[j])
+        if n_lo > 1:
+            arrived(r1a.at[j], s1ar.at[j])
         for e in list(range(1, n_hi)) + [0]:
             h2 = (hi + e) % n_hi
             s = pa[j, h2, lo].astype(F32)
@@ -229,10 +227,10 @@
                 acca[j] = s
             else:
                 s2a[j, e - 1] = s.astype(BF16)
-                send(s2a.at[j, e - 1], r2a.at[j, e - 1], s2as.at[j, e - 1],
-                     s2ar.at[j, e - 1], (gx, h2 * n_lo + lo))
-        for d in range(1, n_hi):
-            first_arrived(r1b.at[j, d - 1], s1br.at[j, d - 1], fb - ca, split[j])
+                send(s2a.at[j, e - 1], r2a.at[j, e - 1], s2as.at[0], s2ar.at[j],
+                     (gx, h2 * n_lo + lo))
+        if n_hi > 1:
+            arrived(r1b.at[j], s1br.at[j])
         for e in list(range(1, n_lo)) + [0]:
             l2 = (lo + e) % n_lo
             s = pb[j, hi, l2].astype(F32)
@@ -242,15 +240,15 @@
                 accb[j] = s
             else:
                 s2b[j, e - 1] = s.astype(BF16)
-                send(s2b.at[j, e - 1], r2b.at[j, e - 1], s2bs.at[j, e - 1],
-                     s2br.at[j, e - 1], (gx, hi * n_lo + l2))
+                send(s2b.at[j, e - 1], r2b.at[j, e - 1], s2bs.at[0], s2br.at[j],
+                     (gx, hi * n_lo + l2))
 
     def activate(job):
         j = job[0]
-        for d in range(1, n_hi):
-            arrived(r2a.at[j, d - 1], s2ar.at[j, d - 1])
-        for d in range(1, n_lo):
-            arrived(r2b.at[j, d - 1], s2br.at[j, d - 1])
+        if n_hi > 1:
+            arrived(r2a.at[j], s2ar.at[j])
+        if n_lo > 1:
+            arrived(r2b.at[j], s2br.at[j])
         for c in range(fb):
             acc, got, peers, at, many = (
                 (acca, r2a, n_hi, c, ca) if c < ca else (accb, r2b, n_lo, c - ca, fb - ca))
@@ -269,7 +267,7 @@
             dest = (hi + a) % n_hi * n_lo + (lo + b) % n_lo
             for q in range(used):
                 a2s[j, at, :, pl.ds(q * BLOCK, BLOCK)] = hid[kept[0, dest, q]]
-            send(a2s.at[j, at], a2r.at[j, gy], xs.at[j, at], xr.at[j, gy], (gx, dest))
+            send(a2s.at[j, at], a2r.at[j, gy], xs.at[0], xr.at[j], (gx, dest))
         for q in range(used):
             a2r[j, gy, :, pl.ds(q * BLOCK, BLOCK)] = hid[kept[0, gy, q]]
 
@@ -277,9 +275,8 @@
 
     def mix(job):
         j = job[0]
-        for d in range(1, n_gy):
-            src = (gy + d) % n_gy
-            arrived(a2r.at[j, src], xr.at[j, src])
+        if n_gy > 1:
+            arrived(a2s.at[j], xr.at[j])
 
         def col(c, _):
             at = pl.multiple_of(c * wide, wide)
@@ -298,19 +295,20 @@
         for d in range(1, per):
             cj = (mc + d) % per
             send(ps.at[j, pl.ds(pl.multiple_of(cj * hr, hr), hr)], fp.at[j, d - 1],
-                 fps.at[j, d - 1], fpr.at[j, d - 1], (zc * per + cj, gy))
+                 fps.at[0], fpr.at[j], (zc * per + cj, gy))
 
     def finish(job):
         j, chip, h = job
         s = ps[j, pl.ds(pl.multiple_of(mc * hr, hr), hr)].astype(F32)
+        if per > 1:
+            arrived(fp.at[j], fpr.at[j])
         for d in range(1, per):
-            arrived(fp.at[j, d - 1], fpr.at[j, d - 1])
             s = s + fp[j, d - 1].astype(F32)
         if j < halves:
             facc[j] = s
         else:
             f2[j] = s.astype(BF16)
-            send(f2.at[j], fr.at[zc, h], fs.at[j], fq.at[zc, h], (chip * per + mc, gy))
+            send(f2.at[j], fr.at[zc, h], fs.at[0], fq.at[zc, h], (chip * per + mc, gy))
 
     def total(h):
         s = facc[h]
@@ -393,6 +391,15 @@
             copy.wait_send()
         else:
             pl.when(when)(copy.wait_send)
+    for many, ref, sem in (
+            (per, gat.at[:, :, 0], None), (n_lo, r1a, s1as), (n_hi, r1b, s1bs),
+            (n_hi, s2a, s2as), (n_lo, s2b, s2bs), (n_gy, a2s, xs), (per, fp, fps),
+            (nc, f2.at[pl.ds(halves, n)], fs)):
+        if many > 1 and sem is not None:
+            left(ref, sem.at[0])
+        elif many > 1:
+            for j in range(1, per):
+                left(ref, ks.at[j - 1])
 
 
 def solution(mesh):
@@ -457,14 +464,14 @@
                 vm((nc, halves, hr, width), BF16),
                 vm((halves, hr, width), F32),
                 dma((8 + halves,)),
-                dma((nc, halves, 1 + per)), dma((nc, halves, per)),
-                dma((jobs, kl, PIECES)), dma((jobs, kl, PIECES)),
-                dma((jobs, kh, PIECES)), dma((jobs, kh, PIECES)),
-                dma((jobs, kh)), dma((jobs, kh)),
-                dma((jobs, kl)), dma((jobs, kl)),
-                dma((jobs, kg)), dma((jobs, n_gy)),
-                dma((jobs,)), dma((nc, halves)),
-                dma((jobs, kp)), dma((jobs, kp)),
+                dma((nc, halves, 2)), dma((kp,)), dma((nc, halves, per)),
+                dma((1,)), dma((jobs,)),
+                dma((1,)), dma((jobs,)),
+                dma((1,)), dma((jobs,)),
+                dma((1,)), dma((jobs,)),
+                dma((1,)), dma((jobs,)),
+                dma((1,)), dma((nc, halves)),
+                dma((1,)), dma((jobs,)),
             ],
             compiler_params=pltpu.CompilerParams(
                 collective_id=0, has_side_effects=True, vmem_limit_bytes=60 * 1024 * 1024),

time: 54.6 us -> 53.1 us (0.973)
  Pallas kernels: 52.4 us -> 50.9 us
    pallas_call x1, Pallas kernels: 52.4 us -> 50.9 us  [body(): pl.pallas_call(functools.partial(kernel, cfg), out_shape=pltpu.VMEM((rows...]
where the time goes in v5:
time: 53.1 us; the launch traced here: 52.9 us
  Pallas kernels  50.9 us (96%)
  between operations  1.3 us (2%)
  local copies, waits for them, and re-layouts  0.66 us (1%)
    pallas_call x1, Pallas kernels, body(): pl.pallas_call(functools.partial(kernel, cfg), out_shape=pltpu.VMEM((rows...  50.9 us

profile of v5, /device:TPU:0, one launch (start us, length us, event | category | flops | bytes accessed | tf_op | source)
XLA Modules:
  0.0 52.9 jit_solution(17627970191798890004)
XLA Ops:
  1.3 50.9 %shard_map.91 = bf16[64,1024]{1,0:T(8,128)(2,1)S(1)} custom-call(s32[2,84]{1,0:T(2,128)} %bitcast.12, s32[1,1]{1,0:T(1,128)S(6)} %copy.12.gct_h, s32[2,48]{1,0:T(2,128)} %bitcast.13, s32[1,1]{1,0:T(1,128)S(6)} %copy.13.dct_h, s32[1,4,8]{2,1,0:T(4,128)} %kept_h.1, bf16[64,1024]{1,0:T(8,128)(2,1)} %tok.1, bf16[84,128,128]{2,1,0:T(8,128)(2,1)} %bitcast.9, ...), custom_call_target="tpu_custom_call" | custom-call | tf_op jit(solution)/shard_map/pallas_call | solution.py:431
  52.3 0.7 %copy.11 = bf16[64,1024]{1,0:T(8,128)(2,1)} copy(bf16[64,1024]{1,0:T(8,128)(2,1)S(1)} %shard_map.91) | data formatting | bytes 262144

commit v6 on v5

--- a/solution.py
+++ b/solution.py
@@ -308,13 +308,14 @@
             facc[j] = s
         else:
             f2[j] = s.astype(BF16)
-            send(f2.at[j], fr.at[zc, h], fs.at[0], fq.at[zc, h], (chip * per + mc, gy))
+            send(f2.at[j], fr.at[zc, h], fs.at[0], fq.at[h], (chip * per + mc, gy))
 
     def total(h):
         s = facc[h]
+        if nc > 1:
+            arrived(fr.at[pl.ds(0, nc - 1), h], fq.at[h])
         for k in range(1, nc):
             c = zc ^ k
-            arrived(fr.at[c, h], fq.at[c, h])
             s = s + fr[c, h].astype(F32)
         out[pl.ds(h * hr, hr)] = s.astype(BF16)
 
@@ -343,9 +344,9 @@
 
     n = len(far)
 
-    def step(stage, i):
+    def step(stage, i, *args):
         if 0 <= i < n:
-            run(stage, far[i])
+            run(stage, far[i], *args)
 
     def more():
         loads[1].wait()
@@ -354,7 +355,7 @@
     run(project, own[0], halves, PIECES, more)
     need(0)
     for i in range(n + 1):
-        step(project, i)
+        step(project, i, 1, PIECES)
         if i == 0:
             loads[2].wait()
             for w in (-1, 1):
@@ -470,7 +471,7 @@
                 dma((1,)), dma((jobs,)),
                 dma((1,)), dma((jobs,)),
                 dma((1,)), dma((jobs,)),
-                dma((1,)), dma((nc, halves)),
+                dma((1,)), dma((halves,)),
                 dma((1,)), dma((jobs,)),
             ],
             compiler_params=pltpu.CompilerParams(

time: 53.1 us -> 53.1 us (level)
  no operation moved by 1% of the time
where the time goes in v6:
time: 53.1 us; the launch traced here: 52.8 us
  Pallas kernels  50.9 us (96%)
  between operations  1.3 us (2%)
  local copies, waits for them, and re-layouts  0.66 us (1%)
    pallas_call x1, Pallas kernels, body(): pl.pallas_call(functools.partial(kernel, cfg), out_shape=pltpu.VMEM((rows...  50.9 us

profile of v6, /device:TPU:0, one launch (start us, length us, event | category | flops | bytes accessed | tf_op | source)
XLA Modules:
  0.0 52.8 jit_solution(10650711484692700162)
XLA Ops:
  1.3 50.9 %shard_map.91 = bf16[64,1024]{1,0:T(8,128)(2,1)S(1)} custom-call(s32[2,84]{1,0:T(2,128)} %bitcast.12, s32[1,1]{1,0:T(1,128)S(6)} %copy.12.gct_h, s32[2,48]{1,0:T(2,128)} %bitcast.13, s32[1,1]{1,0:T(1,128)S(6)} %copy.13.dct_h, s32[1,4,8]{2,1,0:T(4,128)} %kept_h.1, bf16[64,1024]{1,0:T(8,128)(2,1)} %tok.1, bf16[84,128,128]{2,1,0:T(8,128)(2,1)} %bitcast.9, ...), custom_call_target="tpu_custom_call" | custom-call | tf_op jit(solution)/shard_map/pallas_call | solution.py:432
  52.2 0.7 %copy.11 = bf16[64,1024]{1,0:T(8,128)(2,1)} copy(bf16[64,1024]{1,0:T(8,128)(2,1)S(1)} %shard_map.91) | data formatting | bytes 262144

commit v7 on v6

--- a/solution.py
+++ b/solution.py
@@ -135,7 +135,7 @@
         for at, way in enumerate(ways):
             to = zc + way
             fits = (to >= 0) & (to < nc)
-            send(ref, ref, gs.at[c, h, at], gr.at[c, h, mc], (to * per + mc, gy),
+            send(ref, ref, gs.at[nc if at else c, h], gr.at[c, h, mc], (to * per + mc, gy),
                  fits if there is None else there & fits, True)
         for j in range(1, per):
             send(ref, ref, ks.at[j - 1], gr.at[c, h, mc],
@@ -465,7 +465,7 @@
                 vm((nc, halves, hr, width), BF16),
                 vm((halves, hr, width), F32),
                 dma((8 + halves,)),
-                dma((nc, halves, 2)), dma((kp,)), dma((nc, halves, per)),
+                dma((nc + 1, halves)), dma((kp,)), dma((nc, halves, per)),
                 dma((1,)), dma((jobs,)),
                 dma((1,)), dma((jobs,)),
                 dma((1,)), dma((jobs,)),

time: 53.1 us -> 53 us (level)
  no operation moved by 1% of the time
where the time goes in v7:
time: 53 us; the launch traced here: 52.8 us
  Pallas kernels  50.8 us (96%)
  between operations  1.3 us (2%)
  local copies, waits for them, and re-layouts  0.66 us (1%)
    pallas_call x1, Pallas kernels, body(): pl.pallas_call(functools.partial(kernel, cfg), out_shape=pltpu.VMEM((rows...  50.8 us

profile of v7, /device:TPU:0, one launch (start us, length us, event | category | flops | bytes accessed | tf_op | source)
XLA Modules:
  0.0 52.8 jit_solution(6430780378894740825)
XLA Ops:
  1.3 50.8 %shard_map.91 = bf16[64,1024]{1,0:T(8,128)(2,1)S(1)} custom-call(s32[2,84]{1,0:T(2,128)} %bitcast.12, s32[1,1]{1,0:T(1,128)S(6)} %copy.12.gct_h, s32[2,48]{1,0:T(2,128)} %bitcast.13, s32[1,1]{1,0:T(1,128)S(6)} %copy.13.dct_h, s32[1,4,8]{2,1,0:T(4,128)} %kept_h.1, bf16[64,1024]{1,0:T(8,128)(2,1)} %tok.1, bf16[84,128,128]{2,1,0:T(8,128)(2,1)} %bitcast.9, ...), custom_call_target="tpu_custom_call" | custom-call | tf_op jit(solution)/shard_map/pallas_call | solution.py:432
  52.1 0.7 %copy.11 = bf16[64,1024]{1,0:T(8,128)(2,1)} copy(bf16[64,1024]{1,0:T(8,128)(2,1)S(1)} %shard_map.91) | data formatting | bytes 262144
